TPU v7x, 32 devices: a whole 2x2x4 slice. The times are simulated.
32 devices in a mesh: row: 8 (over y, x, core), col: 4 (over z).
Axes of the slice: x: 2, y: 2, z: 4, core: 2. Of those that a mesh axis runs over, the one named last changes fastest.
Arguments:
- a_matrix: float32 [2048, 2048], P('row', 'col'), may hold values from -0.9 to 0.9
- b_matrix: float32 [2048, 2048], P('row', 'col'), may hold values from -0.9 to 0.9
- a_panel: float32 [2048, 1024], P('row', 'col'), may hold values from -0.9 to 0.9
- b_panel: float32 [2048, 1024], P('row', 'col'), may hold values from -0.9 to 0.9
Outputs:
- triangle: float32 [1024, 1024], P('row', 'col')
- pencil_cross: float32 [2048, 2048], P('row', 'col')
All inputs are finite; a program needn't handle non-finite values.
Results may differ from a plain program's by a relative error of at most 0.0003.
Values sent between devices are 32-bit elements; how exact they have to be, the bound alone decides.
No kernel may reach another device: no remote copies, remote signals or barrier semaphores. Data moves between devices by JAX's collectives and lax.ppermute only.
A program may use at most 64 MiB of HBM per device.

v0:
```python
import jax
import jax.numpy as jnp
from jax import lax
from jax.sharding import PartitionSpec as P

HIGHEST = lax.Precision.HIGHEST


def local(a_matrix, b_matrix, a_panel, b_panel):
    row_count = a_matrix.shape[0]
    panel_width = a_panel.shape[1]
    full_a, full_pa, full_pb = (
        lax.all_gather(a_matrix, "col", axis=1, tiled=True),
        lax.all_gather(a_panel, "col", axis=1, tiled=True),
        lax.all_gather(b_panel, "col", axis=1, tiled=True),
    )
    stacked = jnp.concatenate([full_pb, -full_pa], 0)
    own_block = jnp.concatenate([b_panel, -a_panel], 0)
    partial_gram = jnp.dot(own_block.T, stacked, precision=HIGHEST)
    gram_rows = lax.psum(partial_gram, "row")
    gram_matrix = lax.all_gather(gram_rows, "col", axis=0, tiled=True)
    lower_factor = jnp.linalg.cholesky(gram_matrix)
    q_rows = jax.scipy.linalg.solve_triangular(lower_factor, stacked.T, lower=True).T
    upper_rows = q_rows[:row_count]
    lower_rows = q_rows[row_count:]
    row_index = lax.axis_index("row")
    col_index = lax.axis_index("col")
    tri_rows = gram_matrix.shape[0] // lax.axis_size("row")
    corner = lax.dynamic_slice(
        lower_factor, (col_index * panel_width, row_index * tri_rows), (panel_width, tri_rows)
    )
    triangle = corner.T
    partial_z = jnp.dot(lower_rows.T, b_matrix, precision=HIGHEST)
    z_columns = lax.psum(partial_z, "row")
    v_block = jnp.dot(upper_rows, z_columns, precision=HIGHEST)
    pencil_cross = lax.psum_scatter(
        -jnp.dot(full_a.T, v_block, precision=HIGHEST), "row", scatter_dimension=0, tiled=True
    )
    return (triangle, pencil_cross)


def solution(mesh):
    in_specs = (P("row", "col"), P("row", "col"), P("row", "col"), P("row", "col"))
    out_specs = (P("row", "col"), P("row", "col"))
    return jax.shard_map(local, mesh=mesh, in_specs=in_specs, out_specs=out_specs, check_vma=False)
```

profile of v0, /device:TPU:0, one launch (start us, length us, event | category | flops | bytes accessed | tf_op | source)
XLA Modules:
  0.0 741.9 jit_solution(5404969723252647219)
XLA Ops:
  9.7 30.6 %all-gather.7.cloned.1.call-done = f32[256,1024]{1,0:T(8,128)} async-done(((f32[256,256]{1,0:T(8,128)}), f32[256,1024]{1,0:T(8,128)}) %all-gather.7.cloned.1.call-update) | async-done | bytes 1048592 | tf_op jit(solution)/shard_map/all_gather | solution.py:14
  41.6 27.7 %all-gather.5.cloned.1.call-done = f32[256,1024]{1,0:T(8,128)} async-done(((f32[256,256]{1,0:T(8,128)}), f32[256,1024]{1,0:T(8,128)}) %all-gather.5.cloned.1.call-update) | async-done | bytes 1048592 | tf_op jit(solution)/shard_map/all_gather | solution.py:15
  69.3 5.7 fusion.3
  75.1 56.2 %all-reduce.4.cloned.1.call-done = f32[256,1024]{0,1:T(8,128)} async-done(((f32[256,1024]{0,1:T(8,128)}), f32[256,1024]{0,1:T(8,128)}) %all-reduce.4.cloned.1.call-update) | async-done | bytes 1048592 | tf_op jit(solution)/shard_map/psum | solution.py:20
  132.9 79.8 %all-gather.9.cloned.1.call-done = f32[1024,1024]{0,1:T(8,128)} async-done(((f32[256,1024]{0,1:T(8,128)}), f32[1024,1024]{0,1:T(8,128)}) %all-gather.9.cloned.1.call-update) | async-done | bytes 4194320 | tf_op jit(solution)/shard_map/all_gather | solution.py:21
  212.7 5.5 copy.7
  218.2 4.4 fusion
  224.6 11.7 %cholesky.223 = f32[128,128]{1,0:T(8,128)S(1)} custom-call(f32[128,128]{1,0:T(8,128)S(1)} %cholesky.580), custom_call_target="Cholesky" | custom-call | tf_op jit(solution)/shard_map/jit(cholesky)/cholesky | solution.py:22
  238.8 9.8 %custom-call.63 = f32[1,128,128]{1,2,0:T(8,128)S(1)} custom-call(f32[1,128,128]{2,1,0:T(8,128)S(1)} %get-tuple-element.70), custom_call_target="InvertDiagBlocksLowerTriangular" | custom-call | tf_op jit(solution)/shard_map/jit(cholesky)/cholesky | solution.py:22
  252.6 11.9 %cholesky.244 = f32[128,128]{1,0:T(8,128)S(1)} custom-call(f32[128,128]{1,0:T(8,128)S(1)} %cholesky.584), custom_call_target="Cholesky" | custom-call | tf_op jit(solution)/shard_map/jit(cholesky)/cholesky | solution.py:22
  265.1 9.8 %custom-call.64 = f32[1,128,128]{1,2,0:T(8,128)S(1)} custom-call(f32[1,128,128]{2,1,0:T(8,128)S(1)} %get-tuple-element.67), custom_call_target="InvertDiagBlocksLowerTriangular" | custom-call | tf_op jit(solution)/shard_map/jit(cholesky)/cholesky | solution.py:22
  278.3 11.7 %cholesky.468 = f32[128,128]{1,0:T(8,128)S(1)} custom-call(f32[128,128]{1,0:T(8,128)S(1)} %cholesky.589), custom_call_target="Cholesky" | custom-call | tf_op jit(solution)/shard_map/jit(cholesky)/cholesky | solution.py:22
  290.7 9.8 %custom-call.65 = f32[1,128,128]{1,2,0:T(8,128)S(1)} custom-call(f32[1,128,128]{2,1,0:T(8,128)S(1)} %get-tuple-element.64), custom_call_target="InvertDiagBlocksLowerTriangular" | custom-call | tf_op jit(solution)/shard_map/jit(cholesky)/cholesky | solution.py:22
  304.0 12.1 %cholesky.487 = f32[128,128]{1,0:T(8,128)S(1)} custom-call(f32[128,128]{1,0:T(8,128)S(1)} %cholesky.594), custom_call_target="Cholesky" | custom-call | tf_op jit(solution)/shard_map/jit(cholesky)/cholesky | solution.py:22
  316.7 9.8 %custom-call.66 = f32[1,128,128]{1,2,0:T(8,128)S(1)} custom-call(f32[1,128,128]{2,1,0:T(8,128)S(1)} %get-tuple-element.61), custom_call_target="InvertDiagBlocksLowerTriangular" | custom-call | tf_op jit(solution)/shard_map/jit(cholesky)/cholesky | solution.py:22
  330.0 11.7 %cholesky.506 = f32[128,128]{1,0:T(8,128)S(1)} custom-call(f32[128,128]{1,0:T(8,128)S(1)} %cholesky.599), custom_call_target="Cholesky" | custom-call | tf_op jit(solution)/shard_map/jit(cholesky)/cholesky | solution.py:22
  342.4 10.0 %custom-call.67 = f32[1,128,128]{1,2,0:T(8,128)S(1)} custom-call(f32[1,128,128]{2,1,0:T(8,128)S(1)} %get-tuple-element.58), custom_call_target="InvertDiagBlocksLowerTriangular" | custom-call | tf_op jit(solution)/shard_map/jit(cholesky)/cholesky | solution.py:22
  355.6 11.7 %cholesky.526 = f32[128,128]{1,0:T(8,128)S(1)} custom-call(f32[128,128]{1,0:T(8,128)S(1)} %cholesky.604), custom_call_target="Cholesky" | custom-call | tf_op jit(solution)/shard_map/jit(cholesky)/cholesky | solution.py:22
  368.0 9.8 %custom-call.68 = f32[1,128,128]{1,2,0:T(8,128)S(1)} custom-call(f32[1,128,128]{2,1,0:T(8,128)S(1)} %get-tuple-element.55), custom_call_target="InvertDiagBlocksLowerTriangular" | custom-call | tf_op jit(solution)/shard_map/jit(cholesky)/cholesky | solution.py:22
  380.8 11.7 %cholesky.546 = f32[128,128]{1,0:T(8,128)S(1)} custom-call(f32[128,128]{1,0:T(8,128)S(1)} %cholesky.609), custom_call_target="Cholesky" | custom-call | tf_op jit(solution)/shard_map/jit(cholesky)/cholesky | solution.py:22
  393.2 9.8 %custom-call.69 = f32[1,128,128]{1,2,0:T(8,128)S(1)} custom-call(f32[1,128,128]{2,1,0:T(8,128)S(1)} %get-tuple-element.52), custom_call_target="InvertDiagBlocksLowerTriangular" | custom-call | tf_op jit(solution)/shard_map/jit(cholesky)/cholesky | solution.py:22
  405.6 11.7 %cholesky.564 = f32[128,128]{1,0:T(8,128)S(1)} custom-call(f32[128,128]{1,0:T(8,128)S(1)} %convolution_subtract_fusion.13), custom_call_target="Cholesky" | custom-call | tf_op jit(solution)/shard_map/jit(cholesky)/cholesky | solution.py:22
  427.6 6.8 fusion.1
  434.3 27.5 %while.1 = (s32[]{:T(128)}, f32[1024,1024]{1,0:T(8,128)}, s32[8,2]{0,1:T(2,128)S(1)}, f32[8,128,128]{2,1,0:T(8,128)}, s32[]{:T(128)}) while((s32[]{:T(128)}, f32[1024,1024]{1,0:T(8,128)}, s32[8,2]{0,1:T(2,128)S(1)}, f32[8,128,128]{2,1,0:T(8,128)}, s32[]{:T(128)}) %tuple.63), condition=%wide.while_cond, body=%wide.while_body.sunk | while | flops 2 | bytes 132205 | solution.py:23
  461.8 79.8 %custom-call.70 = f32[8,128,128]{1,2,0:T(8,128)S(1)} custom-call(f32[8,128,128]{2,1,0:T(8,128)} %get-tuple-element.9), custom_call_target="InvertDiagBlocksLowerTriangular" | custom-call | tf_op jit(solution)/shard_map/jit(_solve_triangular)/triangular_solve | solution.py:23
  556.2 3.6 convolution_subtract_fusion.7
  560.3 4.3 convolution_subtract_fusion.3
  570.1 59.8 %all-reduce.6.cloned.1.call-done = f32[1024,512]{1,0:T(8,128)} async-done(((f32[1024,512]{1,0:T(8,128)}), f32[1024,512]{1,0:T(8,128)}) %all-reduce.6.cloned.1.call-update) | async-done | bytes 2097168 | tf_op jit(solution)/shard_map/psum | solution.py:34
  629.8 3.5 fusion.6
  633.4 42.7 %all-gather.11.cloned.1.call-done = f32[256,2048]{1,0:T(8,128)} async-done(((f32[256,512]{1,0:T(8,128)}), f32[256,2048]{1,0:T(8,128)}) %all-gather.11.cloned.1.call-update) | async-done | bytes 2097168 | tf_op jit(solution)/shard_map/all_gather | solution.py:13
  676.0 6.7 negate_bitcast_fusion
  684.5 48.3 %reduce-scatter.2.cloned.1.call-done = f32[256,512]{0,1:T(8,128)} async-done(((f32[2048,512]{0,1:T(8,128)}), f32[256,512]{0,1:T(8,128)}) %reduce-scatter.2.cloned.1.call-update) | async-done | bytes 524304 | tf_op jit(solution)/shard_map/reduce_scatter | solution.py:36
  (112 shorter events, 93.8 us)
Async XLA Ops:
  7.2 559.1 %copy-start = (f32[256,512]{1,0:T(8,128)S(1)}, f32[256,512]{1,0:T(8,128)}, u32[]{:S(2)}) copy-start(f32[256,512]{1,0:T(8,128)} %param.5) | copy-start | bytes 1572868
  7.2 62.1 %copy-start.6 = (f32[256,256]{1,0:T(8,128)S(1)}, f32[256,256]{1,0:T(8,128)}, u32[]{:S(2)}) copy-start(f32[256,256]{1,0:T(8,128)} %param.7) | copy-start | bytes 786436
  7.2 33.1 %all-gather.7.cloned.1.call-start = ((), (), s32[]{:S(2)}) async-start(), calls=%async_computation.2 | async-start | bytes 1310720 | tf_op jit(solution)/shard_map/all_gather | solution.py:14
  7.9 61.3 %all-gather.5.cloned.1.call-start = ((), (), s32[]{:S(2)}) async-start(), calls=%async_computation.1 | async-start | bytes 1310720 | tf_op jit(solution)/shard_map/all_gather | solution.py:15
  8.7 122.6 %all-reduce.4.cloned.1.call-start = ((), (), s32[]{:S(2)}) async-start(), calls=%async_computation.3 | async-start | bytes 2097152 | tf_op jit(solution)/shard_map/psum | solution.py:20
  69.3 62.1 %copy-start.3 = (f32[256,1024]{1,0:T(8,128)S(1)}, f32[256,1024]{1,0:T(8,128)}, u32[]{:S(2)}) copy-start(f32[256,1024]{1,0:T(8,128)} %all-gather.5.cloned.1.call-done) | copy-start | bytes 3145732
  75.0 137.7 %all-gather.9.cloned.1.call-start = ((), (), s32[]{:S(2)}) async-start(), calls=%async_computation.4 | async-start | bytes 5242880 | tf_op jit(solution)/shard_map/all_gather | solution.py:21
  131.3 498.5 %all-reduce.6.cloned.1.call-start = ((), (), s32[]{:S(2)}) async-start(), calls=%async_computation.5 | async-start | bytes 4194304 | tf_op jit(solution)/shard_map/psum | solution.py:34
  222.7 1.9 copy-start.1
  427.6 114.1 %copy-start.2 = (f32[1024,512]{0,1:T(8,128)S(1)}, f32[1024,512]{0,1:T(8,128)}, u32[]{:S(2)}) copy-start(f32[1024,512]{0,1:T(8,128)} %fusion.2) | copy-start | bytes 6291460
  565.0 1.3 copy-start.4
  569.4 60.4 %copy-start.5 = (f32[1024,512]{1,0:T(8,128)S(1)}, f32[1024,512]{1,0:T(8,128)}, u32[]{:S(2)}) copy-start(f32[1024,512]{1,0:T(8,128)} %copy-done.4) | copy-start | bytes 6291460
  569.4 106.6 %all-gather.11.cloned.1.call-start = ((), (), s32[]{:S(2)}) async-start(), calls=%async_computation.6 | async-start | bytes 2621440 | tf_op jit(solution)/shard_map/all_gather | solution.py:13
  570.0 162.8 %reduce-scatter.2.cloned.1.call-start = ((), (), s32[]{:S(2)}) async-start(), calls=%async_computation.7 | async-start | bytes 4718592 | tf_op jit(solution)/shard_map/reduce_scatter | solution.py:36
Sparse Core Ops, SparseCore 0:
  9.6 30.6 all-gather.6
  41.9 27.3 all-gather.4
  75.2 56.0 all-reduce.3
  132.7 79.9 all-gather.8
  569.6 60.2 all-reduce.5
  631.3 44.7 all-gather.10
  682.9 49.8 reduce-scatter.1
where the time goes:
time: 747 us; the launch traced here: 742 us
  waiting for transfers between devices  347 us (46%)
  other arithmetic  267 us (36%)
  matrix products  65.4 us (9%)
  local copies, waits for them, and re-layouts  42.5 us (6%)
  between operations  19.6 us (3%)
    another operation x30, other arithmetic, local(): lower_factor = jnp.linalg.cholesky(gram_matrix)  172 us
    another operation x3, other arithmetic, local(): jax.scipy.linalg.solve_triangular(lower_factor, stacked.T, lower=True)  86.6 us
    all_gather x1, waiting for transfers between devices, local(): gram_matrix = lax.all_gather(gram_rows, 'col', axis=0, tiled=True)  79.8 us
    psum x1, waiting for transfers between devices, local(): z_columns = lax.psum(partial_z, 'row')  59.8 us
    psum x1, waiting for transfers between devices, local(): gram_rows = lax.psum(partial_gram, 'row')  56.2 us
    reduce_scatter x1, waiting for transfers between devices, local(): lax.psum_scatter(-jnp.dot(full_a.T, v_block, precision=HIGHEST), 'row', s...  48.3 us
    all_gather x1, waiting for transfers between devices, local(): lax.all_gather(a_matrix, 'col', axis=1, tiled=True)  42.7 us
    all_gather x1, waiting for transfers between devices, local(): lax.all_gather(a_panel, 'col', axis=1, tiled=True)  30.6 us
  transfers between devices with their start and end apart: 7, of which 7 were waited for; matrix products, arithmetic and copies ran while one was open for 1% of the time, Pallas kernels for 0%

commit v1 on v0

v1 whole, which is shorter than its diff:
```python
import jax
import jax.numpy as jnp
from jax import lax
from jax.experimental import pallas as pl
from jax.experimental.pallas import tpu as pltpu
from jax.sharding import PartitionSpec as P

F32 = jnp.float32
BF16 = jnp.bfloat16
HIGHEST = lax.Precision.HIGHEST
NB = 128
SB = 16


def split3(x):
    hi=x.astype(BF16); r=x-hi.astype(F32)
    mid=r.astype(BF16); lo=(r-mid.astype(F32)).astype(BF16)
    return hi,mid,lo
def split2(x):
    hi=x.astype(BF16); lo=(x-hi.astype(F32)).astype(BF16)
    return hi,lo

def factor_block(diag):
    rows=lax.broadcasted_iota(jnp.int32,(NB,NB),0); cols=lax.broadcasted_iota(jnp.int32,(NB,NB),1)
    work=jnp.concatenate([diag,jnp.where(rows==cols,1.0,0.0).astype(F32)],1)
    sub=lax.broadcasted_iota(jnp.int32,(SB,NB),0)
    done=[]
    for s in range(NB//SB):
        j0=s*SB
        block=work[:SB]
        col=[jnp.broadcast_to(block[:,j0+t:j0+t+1],(SB,NB)) for t in range(SB)]
        left,right=block[:,:NB],block[:,NB:]
        scale=jnp.zeros((SB,NB),F32)
        for t in range(SB):
            ct=col[t]
            inv_root=lax.rsqrt(jnp.broadcast_to(ct[t:t+1],(SB,NB)))
            scale=jnp.where(sub==t,inv_root,scale)
            if t==SB-1: break
            mult=jnp.where(sub>t,ct,0.0)*(inv_root*inv_root)
            for u in range(t+1,SB):
                col[u]=col[u]-mult*jnp.broadcast_to(ct[u:u+1],(SB,NB))
            left=left-mult*jnp.broadcast_to(left[t:t+1],(SB,NB))
            right=right-mult*jnp.broadcast_to(right[t:t+1],(SB,NB))
        left=left*scale; right=right*scale
        final=jnp.concatenate([left,right],1)
        done.append(final)
        if s<NB//SB-1:
            hi,mid,lo=split3(final)
            lhs=jnp.concatenate([hi,hi,hi,mid,mid,lo],0)[:,:NB]
            rhs=jnp.concatenate([hi,mid,lo,hi,mid,hi],0)
            upd=lax.dot_general(lhs,rhs,(((0,),(0,)),((),())),preferred_element_type=F32)
            work=work[SB:]-upd[j0+SB:]
    full=jnp.concatenate(done,0)
    return jnp.where(rows<=cols,full[:,:NB],0.0),full[:,NB:]

def chol_kernel(g_ref,r_ref,w_ref):
    k_total=g_ref.shape[0]//NB
    n=g_ref.shape[0]
    for i in range(k_total):
        r_ref[i*NB:(i+1)*NB,i*NB:]=g_ref[i*NB:(i+1)*NB,i*NB:]
        if i: r_ref[i*NB:(i+1)*NB,:i*NB]=jnp.zeros((NB,i*NB),F32)
    for k in range(k_total):
        a,b=k*NB,(k+1)*NB
        fac,inv=factor_block(r_ref[a:b,a:b])
        r_ref[a:b,a:b]=fac
        w_ref[a:b,:]=inv
        if b==n: break
        panel=jnp.dot(inv,r_ref[a:b,b:],precision=HIGHEST,preferred_element_type=F32)
        r_ref[a:b,b:]=panel
        for i in range(k+1,k_total):
            c,d=i*NB,(i+1)*NB
            lhs=panel[:,c-b:d-b]; rhs=panel[:,c-b:]
            r_ref[c:d,c:]=r_ref[c:d,c:]-lax.dot_general(lhs,rhs,(((0,),(0,)),((),())),precision=HIGHEST,preferred_element_type=F32)

def chol(g):
    n=g.shape[0]
    return pl.pallas_call(chol_kernel,out_shape=(jax.ShapeDtypeStruct((n,n),F32),jax.ShapeDtypeStruct((n,NB),F32)),
        name="chol",compiler_params=pltpu.CompilerParams(vmem_limit_bytes=48*2**20))(g)

def solve_kernel(x_ref,r_ref,w_ref,o_ref,v_ref):
    n=r_ref.shape[0]; m=o_ref.shape[0]
    v_ref[...]=x_ref[...]
    NT=(((1,),(1,)),((),()))
    for k in range(n//NB):
        a,b=k*NB,(k+1)*NB
        xh,xl=split2(v_ref[:,a:b]); wh,wl=split2(w_ref[a:b,:])
        vk=lax.dot_general(jnp.concatenate([xh,xh,xl],1),jnp.concatenate([wh,wl,wh],1),NT,preferred_element_type=F32)
        v_ref[:,a:b]=vk
        if b<n:
            vh,vl=split2(vk); rh,rl=split2(r_ref[a:b,b:])
            v_ref[:,b:]=v_ref[:,b:]-jnp.dot(jnp.concatenate([vh,vh,vl],1),jnp.concatenate([rh,rl,rh],0),preferred_element_type=F32)
    vh,vl=split2(v_ref[...])
    o_ref[...]=lax.dot_general(jnp.concatenate([vh[:m],vh[:m],vl[:m]],1),jnp.concatenate([vh[m:],vl[m:],vh[m:]],1),NT,preferred_element_type=F32)

def solve(x,r,w,m):
    return pl.pallas_call(solve_kernel,out_shape=jax.ShapeDtypeStruct((m,x.shape[0]-m),F32),
        scratch_shapes=[pltpu.VMEM(x.shape,F32)],name="solve",
        compiler_params=pltpu.CompilerParams(vmem_limit_bytes=48*2**20))(x,r,w)


TN = (((0,), (0,)), ((), ()))


def local(a_matrix, b_matrix, a_panel, b_panel):
    row_axis, col_axis = lax.axis_size("row"), lax.axis_size("col")
    row_index, col_index = lax.axis_index("row"), lax.axis_index("col")
    rows, width = a_panel.shape
    own = jnp.concatenate([b_panel, a_panel], 0)
    full = lax.all_gather(own, "col", axis=1, tiled=True)
    full_b, full_a = full[:rows], full[rows:]
    order = width * col_axis
    part = lax.dot_general(own, full, TN, precision=HIGHEST)
    share = width // row_axis
    pieces = lax.all_to_all(part.reshape(row_axis, share, order), "row", 0, 0, tiled=True)
    gram_piece = jnp.sum(pieces, 0)
    gram_cols = lax.all_gather(gram_piece, "col", axis=0, tiled=False)
    gram = lax.all_gather(gram_cols, "row", axis=1, tiled=False).reshape(order, order)
    part_x = lax.dot_general(a_matrix, full_b, TN, precision=HIGHEST)
    part_y = lax.dot_general(b_matrix, full_a, TN, precision=HIGHEST)
    x_piece = lax.psum_scatter(part_x, "row", scatter_dimension=0, tiled=True)
    y_rows = lax.psum(part_y, "row")
    ratio = row_axis // col_axis
    moves = [
        (r * col_axis + c, (c * ratio + r // col_axis) * col_axis + r % col_axis)
        for r in range(row_axis)
        for c in range(col_axis)
    ]
    x_piece = lax.ppermute(x_piece, ("row", "col"), moves)
    x_rows = lax.all_gather(x_piece, "col", axis=0, tiled=True)
    upper, inverses = chol(gram)
    both = jnp.concatenate([x_rows, y_rows], 0)
    pencil_cross = solve(both, upper, inverses, x_rows.shape[0])
    tri_rows = order // row_axis
    triangle = lax.dynamic_slice(upper, (row_index * tri_rows, col_index * width), (tri_rows, width))
    return triangle, pencil_cross


def solution(mesh):
    specs = (P("row", "col"),) * 4
    return jax.shard_map(local, mesh=mesh, in_specs=specs, out_specs=(P("row", "col"),) * 2, check_vma=False)
```

time: 747 us -> 297 us (0.40)
  other arithmetic: 267 us -> 4.02 us
  waiting for transfers between devices: 347 us -> 162 us
  matrix products: 65.4 us -> 9.69 us
  blocking collectives: 0 us -> 53.6 us
  Pallas kernels: 0 us -> 45.9 us
  local copies, waits for them, and re-layouts: 42.5 us -> 5.51 us
    another operation x33 -> x0, other arithmetic: 259 us -> none  [the longest x30 172 us: local(): lower_factor = jnp.linalg.cholesky(gram_matrix)]
    psum x2 -> x1, waiting for transfers between devices: 116 us -> 14.3 us  [local(): y_rows = lax.psum(part_y, 'row')]
    all_gather x4 -> x3, waiting for transfers between devices: 181 us -> 111 us  [the longest x1 48.5 us: local(): full = lax.all_gather(own, 'col', axis=1, tiled=True)]
    another operation x29 -> x0, matrix products: 46.3 us -> none  [the longest x15 23.2 us: local(): jax.scipy.linalg.solve_triangular(lower_factor, stacked.T, lower=True)]
    pallas_call x0 -> x2, Pallas kernels: none -> 45.9 us  [the longest x1 37.2 us: chol(): pl.pallas_call(chol_kernel, out_shape=(jax.ShapeDtypeStruct((n, n), F32),...]
    all_to_all x0 -> x1, blocking collectives: none -> 37.3 us  [local(): lax.all_to_all(part.reshape(row_axis, share, order), 'row', 0, 0, tiled=T...]
    another operation x33 -> x0, local copies, waits for them, and re-layouts: 30 us -> none
    all_gather x0 -> x1, blocking collectives: none -> 16.3 us  [local(): gram_cols = lax.all_gather(gram_piece, 'col', axis=0, tiled=False)]
  transfers between devices with their start and end apart: 7 -> 6, of which waited for: 7 -> 5; matrix products, arithmetic and copies ran while one was open for 1% -> 3% of each run, Pallas kernels for 0% -> 0%
where the time goes in v1:
time: 297 us; the launch traced here: 296 us
  waiting for transfers between devices  162 us (55%)
  blocking collectives  53.6 us (18%)
  Pallas kernels  45.9 us (15%)
  between operations  13.9 us (5%)
  matrix products  9.69 us (3%)
  local copies, waits for them, and re-layouts  5.51 us (2%)
  other arithmetic  4.02 us (1%)
    all_gather x1, waiting for transfers between devices, local(): full = lax.all_gather(own, 'col', axis=1, tiled=True)  48.5 us
    all_to_all x1, blocking collectives, local(): lax.all_to_all(part.reshape(row_axis, share, order), 'row', 0, 0, tiled=T...  37.3 us
    pallas_call x1, Pallas kernels, chol(): pl.pallas_call(chol_kernel, out_shape=(jax.ShapeDtypeStruct((n, n), F32),...  37.2 us
    reduce_scatter x1, waiting for transfers between devices, local(): x_piece = lax.psum_scatter(part_x, 'row', scatter_dimension=0, tiled=True)  36.7 us
    all_gather x1, waiting for transfers between devices, local(): lax.all_gather(gram_cols, 'row', axis=1, tiled=False).reshape(order, order)  33.8 us
    all_gather x1, waiting for transfers between devices, local(): x_rows = lax.all_gather(x_piece, 'col', axis=0, tiled=True)  28.5 us
    all_gather x1, blocking collectives, local(): gram_cols = lax.all_gather(gram_piece, 'col', axis=0, tiled=False)  16.3 us
    psum x1, waiting for transfers between devices, local(): y_rows = lax.psum(part_y, 'row')  14.3 us
  transfers between devices with their start and end apart: 6, of which 5 were waited for; matrix products, arithmetic and copies ran while one was open for 3% of the time, Pallas kernels for 0%

profile of v1, /device:TPU:0, one launch (start us, length us, event | category | flops | bytes accessed | tf_op | source)
XLA Modules:
  0.0 296.2 jit_solution(16111485792644670546)
XLA Ops:
  7.2 0.0 copy-start
  7.2 0.0 all-gather.6.cloned.1.call-start
  7.2 1.0 constant_dynamic-update-slice_fusion.1
  8.2 1.0 constant_dynamic-update-slice_fusion
  9.2 0.8 copy-done.4
  10.0 0.0 all-gather.6.cloned.1.call-update
  10.1 0.0 reduce-scatter.2.cloned.1.call-start
  10.1 48.5 %all-gather.6.cloned.1.call-done = f32[512,1024]{1,0:T(8,128)} async-done(((f32[512,256]{1,0:T(8,128)}), f32[512,1024]{1,0:T(8,128)}) %all-gather.6.cloned.1.call-update) | async-done | bytes 2097168 | tf_op jit(solution)/shard_map/all_gather | solution.py:109
  58.6 4.6 %convolution_bitcast_fusion.1 = f32[512,1024]{1,0:T(8,128)} fusion(f32[256,512]{1,0:T(8,128)S(1)} %copy-done, f32[512,1024]{1,0:T(8,128)} %all-gather.6.cloned.1.call-done), kind=kOutput, calls=%fused_computation.2 | convolution fusion | flops 1610612736 | bytes 3670016 | tf_op jit(solution)/shard_map/dot_general | solution.py:118
  63.2 0.0 reduce-scatter.2.cloned.1.call-update
  63.2 0.0 all-reduce.2.cloned.1.call-start
  63.3 3.2 %convolution_bitcast_fusion = f32[512,1024]{1,0:T(8,128)} fusion(f32[256,512]{1,0:T(8,128)S(1)} %copy-done.6, f32[512,1024]{1,0:T(8,128)S(1)} %copy-done.3), kind=kOutput, calls=%fused_computation.1 | convolution fusion | flops 1610612736 | bytes 3670016 | tf_op jit(solution)/shard_map/dot_general | solution.py:119
  66.5 0.0 all-reduce.2.cloned.1.call-update
  66.5 0.0 all-gather.8.cloned.1.call-start
  66.6 36.7 %reduce-scatter.2.cloned.1.call-done = f32[64,1024]{1,0:T(8,128)} async-done(((f32[512,1024]{1,0:T(8,128)}), f32[64,1024]{1,0:T(8,128)}) %reduce-scatter.2.cloned.1.call-update) | async-done | bytes 262160 | tf_op jit(solution)/shard_map/reduce_scatter | solution.py:120
  103.3 1.6 collective-permute-start
  104.9 0.7 copy-done.7
  105.6 0.0 all-gather.8.cloned.1.call-update
  105.6 0.0 all-gather.10.cloned.1.call-start
  105.6 1.9 fusion.2
  107.5 37.3 %all_to_all.5 = f32[8,32,1024]{2,1,0:T(8,128)S(1)} all-to-all(f32[8,32,1024]{2,1,0:T(8,128)S(1)} %bitcast.11), channel_id=1, replica_groups=mesh['row'=8,'col'=4] {'row'}, dimensions={0} | all-to-all | bytes 2097152 | tf_op jit(solution)/shard_map/all_to_all | solution.py:114
  144.8 0.1 reduce_sum.9
  144.9 16.3 %all-gather = f32[128,1024]{1,0:T(8,128)} all-gather(f32[32,1024]{1,0:T(8,128)S(1)} %reduce_sum.9), channel_id=2, replica_groups=mesh['row'=8,'col'=4] {'col'}, dimensions={0}, use_global_device_ids=true | all-gather | bytes 655360 | tf_op jit(solution)/shard_map/all_gather | solution.py:116
  161.2 0.0 all-gather.10.cloned.1.call-update
  161.2 14.3 %all-reduce.2.cloned.1.call-done = f32[512,1024]{1,0:T(8,128)} async-done(((f32[512,1024]{1,0:T(8,128)}), f32[512,1024]{1,0:T(8,128)}) %all-reduce.2.cloned.1.call-update) | async-done | bytes 2097168 | tf_op jit(solution)/shard_map/psum | solution.py:121
  175.5 28.5 %all-gather.8.cloned.1.call-done = f32[256,1024]{1,0:T(8,128)} async-done(((f32[64,1024]{1,0:T(8,128)}), f32[256,1024]{1,0:T(8,128)}) %all-gather.8.cloned.1.call-update) | async-done | bytes 1048592 | tf_op jit(solution)/shard_map/all_gather | solution.py:129
  204.1 4.0 %pad_maximum_fusion.x_ref = f32[768,1024]{1,0:T(8,128)} fusion(f32[512,1024]{1,0:T(8,128)} %all-reduce.2.cloned.1.call-done, f32[256,1024]{1,0:T(8,128)} %all-gather.8.cloned.1.call-done), kind=kLoop, calls=%fused_computation | loop fusion | flops 786432 | bytes 6291456 | tf_op jit(solution)/shard_map/concatenate | solution.py:131
  208.0 33.8 %all-gather.10.cloned.1.call-done = f32[4,256,1024]{2,1,0:T(8,128)} async-done(((f32[4,32,1024]{2,1,0:T(8,128)}), f32[4,256,1024]{2,1,0:T(8,128)}) %all-gather.10.cloned.1.call-update) | async-done | bytes 4194320 | tf_op jit(solution)/shard_map/all_gather | solution.py:117
  241.8 37.2 %chol.1 = (f32[1024,1024]{1,0:T(8,128)S(1)}, f32[1024,128]{1,0:T(8,128)S(1)}) custom-call(f32[1024,1024]{1,0:T(8,128)} %bitcast.12), custom_call_target="tpu_custom_call" | custom-call | tf_op jit(solution)/shard_map/chol/pallas_call | solution.py:77
  279.0 0.7 dynamic_slice.3
  279.8 1.3 copy-done.2
  281.0 8.7 %solve.1 = f32[256,512]{1,0:T(8,128)} custom-call(f32[768,1024]{1,0:T(8,128)S(1)} %copy-done.1, f32[1024,1024]{1,0:T(8,128)} %copy-done.2, f32[1024,128]{1,0:T(8,128)S(1)} %get-tuple-element.5.w_ref), custom_call_target="tpu_custom_call" | custom-call | tf_op jit(solution)/shard_map/solve/pallas_call | solution.py:96
  (13 shorter events, 0.0 us)
Async XLA Ops:
  7.2 51.4 %copy-start = (f32[256,512]{1,0:T(8,128)S(1)}, f32[256,512]{1,0:T(8,128)}, u32[]{:S(2)}) copy-start(f32[256,512]{1,0:T(8,128)} %param.4) | copy-start | bytes 1572868
  7.2 51.4 %all-gather.6.cloned.1.call-start = ((), (), s32[]{:S(2)}) async-start(), calls=%async_computation.2 | async-start | bytes 2621440 | tf_op jit(solution)/shard_map/all_gather | solution.py:109
  9.2 0.8 copy-start.4
  10.0 53.2 %copy-start.6 = (f32[256,512]{1,0:T(8,128)S(1)}, f32[256,512]{1,0:T(8,128)}, u32[]{:S(2)}) copy-start(f32[256,512]{1,0:T(8,128)} %param.5) | copy-start | bytes 1572868
  10.1 93.2 %reduce-scatter.2.cloned.1.call-start = ((), (), s32[]{:S(2)}) async-start(), calls=%async_computation.3 | async-start | bytes 2359296 | tf_op jit(solution)/shard_map/reduce_scatter | solution.py:120
  58.6 4.7 %copy-start.3 = (f32[512,1024]{1,0:T(8,128)S(1)}, f32[512,1024]{1,0:T(8,128)}, u32[]{:S(2)}) copy-start(f32[512,1024]{1,0:T(8,128)} %all-gather.6.cloned.1.call-done) | copy-start | bytes 6291460
  63.2 112.4 %all-reduce.2.cloned.1.call-start = ((), (), s32[]{:S(2)}) async-start(), calls=%async_computation.5 | async-start | bytes 4194304 | tf_op jit(solution)/shard_map/psum | solution.py:121
  66.5 39.1 %copy-start.5 = (f32[512,256]{1,0:T(8,128)S(1)}, f32[512,256]{1,0:T(8,128)}, u32[]{:S(2)}) copy-start(f32[512,256]{1,0:T(8,128)} %copy-done.4) | copy-start | bytes 1572868
  66.5 137.5 %all-gather.8.cloned.1.call-start = ((), (), s32[]{:S(2)}) async-start(), calls=%async_computation.4 | async-start | bytes 1310720 | tf_op jit(solution)/shard_map/all_gather | solution.py:129
  103.3 1.6 collective-permute-start
  104.9 0.7 copy-start.7
  105.6 136.2 %all-gather.10.cloned.1.call-start = ((), (), s32[]{:S(2)}) async-start(), calls=%async_computation.6 | async-start | bytes 4718592 | tf_op jit(solution)/shard_map/all_gather | solution.py:117
  241.8 39.2 %copy-start.1 = (f32[768,1024]{1,0:T(8,128)S(1)}, f32[768,1024]{1,0:T(8,128)}, u32[]{:S(2)}) copy-start(f32[768,1024]{1,0:T(8,128)} %pad_maximum_fusion.x_ref) | copy-start | bytes 9437188
  279.0 2.0 copy-start.2
Sparse Core Ops, SparseCore 0:
  10.2 48.3 all-gather.5
  63.3 39.9 reduce-scatter.1
  106.5 69.0 all-reduce.1
  177.0 27.0 all-gather.7
  205.8 35.9 all-gather.9
